TPU v7x, 32 devices: a whole 2x2x4 slice. The times are simulated.
32 devices in a mesh: rep: 16 (over z, y, x), shard: 2 (over core).
Axes of the slice: x: 2, y: 2, z: 4, core: 2. Of those that a mesh axis runs over, the one named last changes fastest.
Arguments:
- params: float32 [16, 1600, 3200], P('rep', None, 'shard'), may hold values from -6 to 6
- momentum: float32 [16, 1600, 3200], P('rep', None, 'shard'), may hold values from -6 to 6
- tokens: bfloat16 [16, 2, 256, 1600], P('rep', None, 'shard'), may hold values from -6 to 6
- targets: bfloat16 [16, 2, 256, 3200], P('rep', None, None, 'shard'), may hold values from -6 to 6
- blend_weight: float32 [3200], P('shard'), may hold values from 0.2 to 0.9
Outputs:
- averaged: float32 [1600, 3200], P(None, 'shard')
- blended: float32 [16, 1600, 3200], P('rep', None, 'shard')
All inputs are finite; a program needn't handle non-finite values.
Results may differ from a plain program's by a relative error of at most 0.0045.
Values may be sent and summed in bfloat16 or wider, within the bound.
A program may use at most 128 MiB of HBM per device.

v0:
```python
import jax
import jax.numpy as jnp
from jax import lax
from jax.sharding import PartitionSpec as P

D = 1600


learn_rate = 0.05
momentum_decay = 0.9


def gelu_tanh(value):
    return jax.nn.gelu(value, approximate=True)


def local(params, momentum, tokens, targets, blend_weight):
    inputs = lax.all_gather(tokens[0], "shard", axis=1, tiled=True)
    wanted = targets[0]
    weight = params[0]
    moment = momentum[0]
    scaling = 1.0 / jnp.sqrt(jnp.float32(D))
    for local_step in range(inputs.shape[0]):
        weight_half = weight.astype(jnp.bfloat16)
        pre = jnp.dot(inputs[local_step], weight_half, preferred_element_type=jnp.float32) * scaling
        activation, pullback = jax.vjp(gelu_tanh, pre)
        (slope,) = pullback(activation - wanted[local_step].astype(jnp.float32))
        hidden_grad = (slope * scaling).astype(jnp.bfloat16)
        gradient = lax.dot_general(
            inputs[local_step],
            hidden_grad,
            (((0,), (0,)), ((), ())),
            preferred_element_type=jnp.float32,
        )
        moment = momentum_decay * moment + gradient
        weight = weight - learn_rate * moment
    replicas = lax.axis_size("rep")
    sum_weight, sum_moment = (
        lax.psum_scatter(weight, "rep", scatter_dimension=0, tiled=True),
        lax.psum_scatter(moment, "rep", scatter_dimension=0, tiled=True),
    )
    averaged, mean_moment = (
        lax.all_gather(sum_weight / jnp.float32(replicas), "rep", axis=0, tiled=True),
        lax.all_gather(sum_moment / jnp.float32(replicas), "rep", axis=0, tiled=True),
    )
    blended = blend_weight * mean_moment + (1.0 - blend_weight) * moment
    return (averaged, blended[None])


def solution(mesh):
    return jax.shard_map(
        local,
        mesh=mesh,
        in_specs=(
            P("rep", None, "shard"),
            P("rep", None, "shard"),
            P("rep", None, "shard", None),
            P("rep", None, None, "shard"),
            P("shard"),
        ),
        out_specs=(P(None, "shard"), P("rep", None, "shard")),
        check_vma=False,
    )
```

profile of v0, /device:TPU:0, one launch (start us, length us, event | category | flops | bytes accessed | tf_op | source)
XLA Modules:
  0.0 943.1 jit_solution(2488638459939863416)
XLA Ops:
  7.2 0.0 all-gather.7.cloned.1.call-start
  7.2 0.7 all-gather.7.cloned.1.call-update
  7.9 0.0 all-reduce.5.cloned.1.call-start
  7.9 13.3 %copy.18 = f32[1,1600,1600]{1,2,0:T(8,128)} copy(f32[1,1600,1600]{2,1,0:T(8,128)} %param.6) | data formatting | bytes 20480000 | tf_op args[1]
  21.2 0.0 copy-start.1
  21.2 13.2 %copy.17 = f32[1,1600,1600]{1,2,0:T(8,128)} copy(f32[1,1600,1600]{2,1,0:T(8,128)} %param.5) | data formatting | bytes 20480000 | tf_op args[0]
  34.5 0.0 all-gather.7.cloned.1.call-done
  34.5 0.0 copy-done.1
  34.5 0.0 copy-start
  34.5 18.9 %bitcast_add_fusion.1 = f32[1600,1600]{0,1:T(8,128)} fusion(f32[1,1600,1600]{1,2,0:T(8,128)} %copy.18, f32[1,1600,1600]{2,1,0:T(8,128)} %param.5, bf16[1,2,256,1600]{2,3,1,0:T(8,128)(2,1)} %all-gather.7.cloned.1.call-done, bf16[1,2,256,1600]{2,3,1,0:T(8,128)(2,1)S(1)} %copy-done.1), kind=kOutput, calls=%fused_computation.1 | convolution fusion | flops 2639360000 | bytes 33177600 | tf_op jit(solution)/shard_map/dot_general | solution.py:29
  53.3 0.0 copy-done
  53.3 27.3 %multiply_subtract_fusion = (f32[1600,1600]{0,1:T(8,128)}, f32[1600,1600]{0,1:T(8,128)}) fusion(f32[1600,1600]{0,1:T(8,128)} %bitcast_add_fusion.1, f32[1,1600,1600]{1,2,0:T(8,128)} %copy.17, bf16[1,2,256,1600]{2,3,1,0:T(8,128)(2,1)S(1)} %copy-done, bf16[1,2,256,1600]{2,3,1,0:T(8,128)(2,1)S(1)} %copy-done.1), kind=kOutput, calls=%fused_computation.4 | convolution fusion | flops 2654720000 | bytes 65536000 | tf_op jit(solution)/shard_map/dot_general | solution.py:29
  80.7 0.0 copy-start.3
  80.7 0.0 all-reduce.5.cloned.1.call-update
  80.7 0.0 all-gather.11.cloned.1.call-start
  80.7 0.6 copy-done.3
  81.3 0.6 dynamic-slice
  82.5 565.9 %all-reduce.5.cloned.1.call-done = (f32[1600,1600]{0,1:T(8,128)}, f32[1600,1600]{0,1:T(8,128)}) async-done(((f32[1600,1600]{0,1:T(8,128)}, f32[1600,1600]{0,1:T(8,128)}), (f32[1600,1600]{0,1:T(8,128)}, f32[1600,1600]{0,1:T(8,128)})) %all-reduce.5.cloned.1.call-update) | async-done | bytes 20480016
  648.5 1.7 fusion.40
  650.2 1.2 copy.20
  651.4 0.0 all-gather.11.cloned.1.call-update
  651.4 0.0 all-gather.9.cloned.1.call-start
  651.4 0.0 copy-start.2
  651.4 1.7 fusion.41
  653.2 1.2 copy.19
  654.3 0.0 all-gather.9.cloned.1.call-update
  654.4 0.0 copy-done.2
  654.4 133.9 %all-gather.11.cloned.1.call-done = f32[16,100,1600]{2,1,0:T(8,128)} async-done(((f32[1,100,1600]{2,1,0:T(8,128)}), f32[16,100,1600]{2,1,0:T(8,128)}) %all-gather.11.cloned.1.call-update) | async-done | bytes 10240016 | tf_op jit(solution)/shard_map/all_gather | solution.py:44
  788.3 10.5 %reshape.27 = f32[1600,1600]{1,0:T(8,128)} reshape(f32[16,100,1600]{2,1,0:T(8,128)} %all-gather.11.cloned.1.call-done) | data formatting | bytes 20480000
  798.8 13.1 %copy.21 = f32[1600,1600]{0,1:T(8,128)} copy(f32[1600,1600]{1,0:T(8,128)} %reshape.27) | data formatting | bytes 20480000
  811.9 12.0 %add_bitcast_fusion = f32[1,1600,1600]{1,2,0:T(8,128)} fusion(f32[1600,1600]{0,1:T(8,128)} %get-tuple-element.11, f32[1600,1600]{0,1:T(8,128)} %copy.21, f32[1600]{0:T(1024)S(1)} %broadcast_subtract_fusion, f32[1600]{0:T(1024)S(1)} %copy-done.2), kind=kLoop, calls=%fused_computation.3 | loop fusion | flops 7680000 | bytes 30732800 | tf_op jit(solution)/shard_map/broadcast_in_dim | solution.py:47
  824.0 13.1 %copy.22 = f32[1,1600,1600]{2,1,0:T(8,128)} copy(f32[1,1600,1600]{1,2,0:T(8,128)} %add_bitcast_fusion) | data formatting | bytes 20480000
  837.1 89.0 %all-gather.9.cloned.1.call-done = f32[16,100,1600]{2,1,0:T(8,128)} async-done(((f32[1,100,1600]{2,1,0:T(8,128)}), f32[16,100,1600]{2,1,0:T(8,128)}) %all-gather.9.cloned.1.call-update) | async-done | bytes 10240016 | tf_op jit(solution)/shard_map/all_gather | solution.py:43
  926.1 10.5 %reshape.25 = f32[1600,1600]{1,0:T(8,128)} reshape(f32[16,100,1600]{2,1,0:T(8,128)} %all-gather.9.cloned.1.call-done) | data formatting | bytes 20480000
  (1 shorter events, 0.0 us)
Async XLA Ops:
  7.2 27.3 %all-gather.7.cloned.1.call-start = ((), (), s32[]{:S(2)}) async-start(), calls=%async_computation | async-start | bytes 2457600 | tf_op jit(solution)/shard_map/all_gather | solution.py:18
  7.9 640.6 %all-reduce.5.cloned.1.call-start = ((), (), s32[]{:S(2)}) async-start(), calls=%async_computation.3 | async-start | bytes 42598400
  21.2 13.2 %copy-start.1 = (bf16[1,2,256,1600]{2,3,1,0:T(8,128)(2,1)S(1)}, bf16[1,2,256,1600]{2,3,1,0:T(8,128)(2,1)}, u32[]{:S(2)}) copy-start(bf16[1,2,256,1600]{2,3,1,0:T(8,128)(2,1)} %param.8) | copy-start | bytes 4915204
  34.5 18.9 %copy-start = (bf16[1,2,256,1600]{2,3,1,0:T(8,128)(2,1)S(1)}, bf16[1,2,256,1600]{2,3,1,0:T(8,128)(2,1)}, u32[]{:S(2)}) copy-start(bf16[1,2,256,1600]{2,3,1,0:T(8,128)(2,1)} %all-gather.7.cloned.1.call-done) | copy-start | bytes 4915204
  80.7 0.7 copy-start.3
  80.7 707.6 %all-gather.11.cloned.1.call-start = ((), (), s32[]{:S(2)}) async-start(), calls=%async_computation.2 | async-start | bytes 11767808 | tf_op jit(solution)/shard_map/all_gather | solution.py:44
  651.4 274.7 %all-gather.9.cloned.1.call-start = ((), (), s32[]{:S(2)}) async-start(), calls=%async_computation.1 | async-start | bytes 11767808 | tf_op jit(solution)/shard_map/all_gather | solution.py:43
  651.4 2.9 copy-start.2
Sparse Core Ops, SparseCore 0:
  9.5 12.2 all-gather.6
  80.8 567.6 all-reduce.4
  651.7 136.4 all-gather.10
  790.8 135.2 all-gather.8
where the time goes:
time: 945 us; the launch traced here: 943 us
  waiting for transfers between devices  789 us (83%)
  local copies, waits for them, and re-layouts  77.3 us (8%)
  matrix products  46.2 us (5%)
  other arithmetic  15.4 us (2%)
  between operations  14.5 us (2%)
    unnamed x5, waiting for transfers between devices  567 us
    all_gather x1, waiting for transfers between devices, local(): lax.all_gather(sum_moment / jnp.float32(replicas), 'rep', axis=0, tiled=T...  134 us
    all_gather x1, waiting for transfers between devices, local(): lax.all_gather(sum_weight / jnp.float32(replicas), 'rep', axis=0, tiled=T...  89 us
    unnamed x17, local copies, waits for them, and re-layouts  77.3 us
    dot_general x2, matrix products, local(): lax.dot_general(inputs[local_step], hidden_grad, (((0,), (0,)), ((), ()))...  46.2 us
  transfers between devices with their start and end apart: 4, of which 3 were waited for; matrix products, arithmetic and copies ran while one was open for 8% of the time, Pallas kernels for 0%

commit v1 on v0

--- a/solution.py
+++ b/solution.py
@@ -1,17 +1,199 @@
+import functools
+
 import jax
 import jax.numpy as jnp
 from jax import lax
+from jax.experimental import pallas as pl
+from jax.experimental.pallas import tpu as pltpu
 from jax.sharding import PartitionSpec as P
-
-D = 1600
-
 
 learn_rate = 0.05
 momentum_decay = 0.9
+ROWS = 8
 
 
 def gelu_tanh(value):
     return jax.nn.gelu(value, approximate=True)
+
+
+def bit_order(chunk, bits):
+    lead = chunk % 3
+    wave = chunk // 3
+    rest = list(range(bits))
+    if lead == 0 or bits < 3:
+        return rest
+    if lead == 1:
+        return [1, 0] + rest[2:]
+    return [2] + ([0, 1] if wave % 2 == 0 else [1, 0]) + rest[3:]
+
+
+def pieces(first, count, split, total):
+    out = []
+    for which, (low, high) in enumerate(((0, split), (split, total))):
+        begin, end = max(first, low), min(first + count, high)
+        if begin < end:
+            out.append((which, begin - low, begin - first, end - begin))
+    return out
+
+
+def mean_kernel(n, bits, chunks, weight_hbm, moment_hbm, out_w_hbm, out_m_hbm,
+                held, staged, landed, result, load_sem, send_sem, recv_sem, store_sem):
+    me = lax.axis_index("rep")
+    sources, sinks = (weight_hbm, moment_hbm), (out_w_hbm, out_m_hbm)
+    split = weight_hbm.shape[0]
+    total = 2 * split
+
+    def side(bit):
+        return (me // (1 << bit)) % 2
+
+    def partner(bit):
+        return me + (1 - 2 * side(bit)) * (1 << bit)
+
+    loads = []
+    for chunk in range(chunks):
+        mine = []
+        for which, at, offset, count in pieces(chunk * n, n, split, total):
+            mine.append(pltpu.make_async_copy(
+                sources[which].at[pl.ds(at, count)],
+                held.at[pl.ds(chunk * n + offset, count)],
+                load_sem.at[chunk, which],
+            ))
+        for copy in mine:
+            copy.start()
+        loads.append(mine)
+    padding = chunks * n - total
+    if padding:
+        held[pl.ds(total, padding)] = jnp.zeros((padding,) + held.shape[1:], held.dtype)
+
+    barrier = pltpu.get_barrier_semaphore()
+    for bit in range(bits):
+        pl.semaphore_signal(barrier, inc=1, device_id={"rep": partner(bit)},
+                            device_id_type=pl.DeviceIdType.MESH)
+    pl.semaphore_wait(barrier, bits)
+
+    copies = {}
+    low = {chunk: [chunk * n] for chunk in range(chunks)}
+
+    def act(chunk, stage):
+        order = bit_order(chunk, bits)
+        if stage == 0:
+            for copy in loads[chunk]:
+                copy.wait()
+        else:
+            copies[chunk, stage - 1].wait_recv()
+        if stage < bits:
+            bit = order[stage]
+            half = n >> (stage + 1)
+            start = low[chunk][stage]
+            keep = start + side(bit) * half
+            give = start + (1 - side(bit)) * half
+            slot = chunk * n + (n - 2 * half)
+            before = slot - 2 * half
+
+            def step(i, carry):
+                if stage == 0:
+                    staged[slot + i] = held[give + i].astype(jnp.bfloat16)
+                else:
+                    staged[slot + i] = (
+                        held[give + i]
+                        + landed[before + (give - start) + i].astype(jnp.float32)
+                    ).astype(jnp.bfloat16)
+                return carry
+
+            def keep_step(i, carry):
+                held[keep + i] = held[keep + i] + landed[before + (keep - start) + i].astype(jnp.float32)
+                return carry
+
+            lax.fori_loop(0, half, step, 0)
+            copy = pltpu.make_async_remote_copy(
+                src_ref=staged.at[pl.ds(slot, half)],
+                dst_ref=landed.at[pl.ds(slot, half)],
+                send_sem=send_sem.at[chunk, stage],
+                recv_sem=recv_sem.at[chunk, stage],
+                device_id={"rep": partner(bit)},
+                device_id_type=pl.DeviceIdType.MESH,
+            )
+            copy.start()
+            copies[chunk, stage] = copy
+            if stage > 0:
+                lax.fori_loop(0, half, keep_step, 0)
+            low[chunk].append(keep)
+        elif stage < 2 * bits:
+            back = 2 * bits - 1 - stage
+            bit = order[back]
+            size = n >> (back + 1)
+            start = low[chunk][back + 1]
+            if stage == bits:
+                slot = chunk * n + n - 2
+                result[start] = (
+                    (held[start] + landed[slot].astype(jnp.float32)) * (1.0 / n)
+                ).astype(jnp.bfloat16)
+            copy = pltpu.make_async_remote_copy(
+                src_ref=result.at[pl.ds(start, size)],
+                dst_ref=result.at[pl.ds(start, size)],
+                send_sem=send_sem.at[chunk, stage],
+                recv_sem=recv_sem.at[chunk, stage],
+                device_id={"rep": partner(bit)},
+                device_id_type=pl.DeviceIdType.MESH,
+            )
+            copy.start()
+            copies[chunk, stage] = copy
+        else:
+            for which, at, offset, count in pieces(chunk * n, n, split, total):
+                copy = pltpu.make_async_copy(
+                    result.at[pl.ds(chunk * n + offset, count)],
+                    sinks[which].at[pl.ds(at, count)],
+                    store_sem.at[chunk, which],
+                )
+                copy.start()
+                stores.append(copy)
+
+    stores = []
+    waves = -(-chunks // 3)
+    for tick in range(waves + 2 * bits):
+        for stage in range(2 * bits, -1, -1):
+            wave = tick - stage
+            if 0 <= wave < waves:
+                for chunk in range(3 * wave, min(3 * wave + 3, chunks)):
+                    act(chunk, stage)
+    for copy in copies.values():
+        copy.wait_send()
+    for copy in stores:
+        copy.wait()
+
+
+def replica_means(weight, moment):
+    n = lax.axis_size("rep")
+    bits = n.bit_length() - 1
+    assert n == 1 << bits
+    rows, columns = weight.shape
+    slabs = rows // ROWS
+    chunks = -(-2 * slabs // n)
+    space = chunks * n
+    shape = (slabs, ROWS, columns)
+    out = jax.ShapeDtypeStruct(shape, jnp.bfloat16)
+    sent = chunks * 2 * (n - 1) * ROWS * columns * 2
+    means = pl.pallas_call(
+        functools.partial(mean_kernel, n, bits, chunks),
+        out_shape=(out, out),
+        in_specs=[pl.BlockSpec(memory_space=pl.ANY)] * 2,
+        out_specs=(pl.BlockSpec(memory_space=pl.ANY),) * 2,
+        scratch_shapes=[
+            pltpu.VMEM((space, ROWS, columns), jnp.float32),
+            pltpu.VMEM((space, ROWS, columns), jnp.bfloat16),
+            pltpu.VMEM((space, ROWS, columns), jnp.bfloat16),
+            pltpu.VMEM((space, ROWS, columns), jnp.bfloat16),
+            pltpu.SemaphoreType.DMA((chunks, 2)),
+            pltpu.SemaphoreType.DMA((chunks, 2 * bits)),
+            pltpu.SemaphoreType.DMA((chunks, 2 * bits)),
+            pltpu.SemaphoreType.DMA((chunks, 2)),
+        ],
+        compiler_params=pltpu.CompilerParams(
+            collective_id=0, has_side_effects=True, vmem_limit_bytes=62 * 1024 * 1024
+        ),
+        cost_estimate=pl.CostEstimate(flops=0, bytes_accessed=sent, transcendentals=0),
+    )(weight.reshape(shape), moment.reshape(shape))
+    return tuple(mean.reshape(rows, columns).astype(jnp.float32) for mean in means)
 
 
 def local(params, momentum, tokens, targets, blend_weight):
@@ -19,7 +201,7 @@
     wanted = targets[0]
     weight = params[0]
     moment = momentum[0]
-    scaling = 1.0 / jnp.sqrt(jnp.float32(D))
+    scaling = 1.0 / jnp.sqrt(jnp.float32(weight.shape[0]))
     for local_step in range(inputs.shape[0]):
         weight_half = weight.astype(jnp.bfloat16)
         pre = jnp.dot(inputs[local_step], weight_half, preferred_element_type=jnp.float32) * scaling
@@ -34,15 +216,7 @@
         )
         moment = momentum_decay * moment + gradient
         weight = weight - learn_rate * moment
-    replicas = lax.axis_size("rep")
-    sum_weight, sum_moment = (
-        lax.psum_scatter(weight, "rep", scatter_dimension=0, tiled=True),
-        lax.psum_scatter(moment, "rep", scatter_dimension=0, tiled=True),
-    )
-    averaged, mean_moment = (
-        lax.all_gather(sum_weight / jnp.float32(replicas), "rep", axis=0, tiled=True),
-        lax.all_gather(sum_moment / jnp.float32(replicas), "rep", axis=0, tiled=True),
-    )
+    averaged, mean_moment = replica_means(weight, moment)
     blended = blend_weight * mean_moment + (1.0 - blend_weight) * moment
     return (averaged, blended[None])
 

time: 945 us -> 273 us (0.29)
  waiting for transfers between devices: 789 us -> 13.9 us
  Pallas kernels: 0 us -> 170 us
  local copies, waits for them, and re-layouts: 77.3 us -> 0.01 us
  other arithmetic: 15.4 us -> 34.3 us
    unnamed x5 -> x1, waiting for transfers between devices: 567 us -> 0.68 us
    all_gather x2 -> x0, waiting for transfers between devices: 223 us -> none  [the longest x1 134 us: local(): lax.all_gather(sum_moment / jnp.float32(replicas), 'rep', axis=0, tiled=T...]
    pallas_call x0 -> x1, Pallas kernels: none -> 170 us  [replica_means(): pl.pallas_call(functools.partial(mean_kernel, n, bits, chunks), out_shape...]
    unnamed x17 -> x6, local copies, waits for them, and re-layouts: 77.3 us -> 0.01 us
    reshape x0 -> x1, other arithmetic: none -> 15.2 us  [replica_means(): weight.reshape(shape)]
    all_gather x1, waiting for transfers between devices: 0.01 us -> 13.2 us  [local(): inputs = lax.all_gather(tokens[0], 'shard', axis=1, tiled=True)]
  transfers between devices with their start and end apart: 4 -> 1, of which waited for: 3 -> 1; matrix products, arithmetic and copies ran while one was open for 8% -> 0% of each run, Pallas kernels for 0% -> 0%
where the time goes in v1:
time: 273 us; the launch traced here: 272 us
  Pallas kernels  170 us (62%)
  matrix products  39.6 us (15%)
  other arithmetic  34.3 us (13%)
  between operations  14 us (5%)
  waiting for transfers between devices  13.9 us (5%)
    pallas_call x1, Pallas kernels, replica_means(): pl.pallas_call(functools.partial(mean_kernel, n, bits, chunks), out_shape...  170 us
    dot_general x2, matrix products, local(): lax.dot_general(inputs[local_step], hidden_grad, (((0,), (0,)), ((), ()))...  39.6 us
    reshape x1, other arithmetic, replica_means(): weight.reshape(shape)  15.2 us
    all_gather x1, waiting for transfers between devices, local(): inputs = lax.all_gather(tokens[0], 'shard', axis=1, tiled=True)  13.2 us
    broadcast_in_dim x1, other arithmetic, local(): return (averaged, blended[None])  11.1 us
    convert_element_type x1, other arithmetic, replica_means(): mean.reshape(rows, columns).astype(jnp.float32)  7.34 us
  transfers between devices with their start and end apart: 1, of which 1 were waited for; matrix products, arithmetic and copies ran while one was open for 0% of the time, Pallas kernels for 0%

profile of v1, /device:TPU:0, one launch (start us, length us, event | category | flops | bytes accessed | tf_op | source)
XLA Modules:
  0.0 272.4 jit_solution(11543696112580521323)
XLA Ops:
  7.2 0.0 all-gather.3.cloned.1.call-start
  7.2 0.7 all-gather.3.cloned.1.call-update
  7.9 0.7 broadcast_subtract_fusion
  8.6 0.0 copy-start.1
  8.6 13.2 %all-gather.3.cloned.1.call-done = bf16[1,2,256,1600]{2,3,1,0:T(8,128)(2,1)} async-done(((bf16[1,2,128,1600]{2,3,1,0:T(8,128)(2,1)}), bf16[1,2,256,1600]{2,3,1,0:T(8,128)(2,1)}) %all-gather.3.cloned.1.call-update) | async-done | bytes 1638416 | tf_op jit(solution)/shard_map/all_gather | solution.py:200
  21.8 0.0 copy-start
  21.8 18.6 %bitcast_add_fusion.1 = f32[1600,1600]{1,0:T(8,128)} fusion(f32[1,1600,1600]{2,1,0:T(8,128)} %param.6, f32[1,1600,1600]{2,1,0:T(8,128)} %param.5, bf16[1,2,256,1600]{2,3,1,0:T(8,128)(2,1)} %all-gather.3.cloned.1.call-done, bf16[1,2,256,1600]{2,3,1,0:T(8,128)(2,1)} %param.8), kind=kOutput, calls=%fused_computation.4 | convolution fusion | flops 2639360000 | bytes 33996800 | tf_op jit(solution)/shard_map/dot_general | solution.py:211
  40.4 0.0 copy-done.1
  40.4 0.0 copy-done
  40.4 21.0 %bitcast_add_fusion = f32[1600,1600]{1,0:T(8,128)} fusion(f32[1600,1600]{1,0:T(8,128)} %bitcast_add_fusion.1, f32[1,1600,1600]{2,1,0:T(8,128)} %param.5, bf16[1,2,256,1600]{2,3,1,0:T(8,128)(2,1)S(1)} %copy-done, bf16[1,2,256,1600]{2,3,1,0:T(8,128)(2,1)S(1)} %copy-done.1), kind=kOutput, calls=%fused_computation.3 | convolution fusion | flops 2644480000 | bytes 44646400 | tf_op jit(solution)/shard_map/dot_general | solution.py:211
  61.4 15.2 %subtract_bitcast_fusion.weight_hbm = f32[200,8,1600]{2,1,0:T(8,128)} fusion(f32[1600,1600]{1,0:T(8,128)} %bitcast_add_fusion, f32[1600,1600]{1,0:T(8,128)} %bitcast_add_fusion.1, f32[1,1600,1600]{2,1,0:T(8,128)} %param.5), kind=kLoop, calls=%fused_computation.6 | loop fusion | flops 10240000 | bytes 40960000 | tf_op jit(solution)/shard_map/reshape | solution.py:195
  76.6 170.5 %shard_map.68 = (bf16[200,8,1600]{2,1,0:T(8,128)(2,1)}, bf16[200,8,1600]{2,1,0:T(8,128)(2,1)}) custom-call(f32[200,8,1600]{2,1,0:T(8,128)} %subtract_bitcast_fusion.weight_hbm, f32[200,8,1600]{2,1,0:T(8,128)} %bitcast.67), custom_call_target="tpu_custom_call" | custom-call | bytes 19200000 | tf_op jit(solution)/shard_map/pallas_call | solution.py:176
  247.1 0.0 copy-start.2
  247.1 7.3 %bitcast_convert_fusion = f32[1600,1600]{1,0:T(8,128)} fusion(bf16[200,8,1600]{2,1,0:T(8,128)(2,1)} %get-tuple-element.4), kind=kLoop, calls=%fused_computation.7 | loop fusion | flops 2560000 | bytes 15360000 | tf_op jit(solution)/shard_map/convert_element_type | solution.py:196
  254.5 0.0 copy-done.2
  254.5 11.1 %fusion.1 = f32[1,1600,1600]{2,1,0:T(8,128)} fusion(f32[1600,1600]{1,0:T(8,128)} %bitcast_add_fusion, bf16[200,8,1600]{2,1,0:T(8,128)(2,1)} %get-tuple-element.5, f32[1600]{0:T(1024)S(1)} %broadcast_subtract_fusion, f32[1600]{0:T(1024)S(1)} %copy-done.2), kind=kLoop, calls=%fused_computation.2 | loop fusion | flops 10240000 | bytes 25612800 | tf_op jit(solution)/shard_map/broadcast_in_dim | solution.py:221
Async XLA Ops:
  7.2 14.6 %all-gather.3.cloned.1.call-start = ((), (), s32[]{:S(2)}) async-start(), calls=%async_computation | async-start | bytes 2457600 | tf_op jit(solution)/shard_map/all_gather | solution.py:200
  8.6 31.8 %copy-start.1 = (bf16[1,2,256,1600]{2,3,1,0:T(8,128)(2,1)S(1)}, bf16[1,2,256,1600]{2,3,1,0:T(8,128)(2,1)}, u32[]{:S(2)}) copy-start(bf16[1,2,256,1600]{2,3,1,0:T(8,128)(2,1)} %param.8) | copy-start | bytes 4915204
  21.8 18.6 %copy-start = (bf16[1,2,256,1600]{2,3,1,0:T(8,128)(2,1)S(1)}, bf16[1,2,256,1600]{2,3,1,0:T(8,128)(2,1)}, u32[]{:S(2)}) copy-start(bf16[1,2,256,1600]{2,3,1,0:T(8,128)(2,1)} %all-gather.3.cloned.1.call-done) | copy-start | bytes 4915204
  247.1 7.4 %copy-start.2 = (f32[1600]{0:T(1024)S(1)}, f32[1600]{0:T(1024)}, u32[]{:S(2)}) copy-start(f32[1600]{0:T(1024)} %param.9) | copy-start | bytes 19204
Sparse Core Ops, SparseCore 0:
  9.5 12.2 all-gather.2

commit v2 on v1

--- a/solution.py
+++ b/solution.py
@@ -10,10 +10,6 @@
 learn_rate = 0.05
 momentum_decay = 0.9
 ROWS = 8
-
-
-def gelu_tanh(value):
-    return jax.nn.gelu(value, approximate=True)
 
 
 def bit_order(chunk, bits):
@@ -196,26 +192,116 @@
     return tuple(mean.reshape(rows, columns).astype(jnp.float32) for mean in means)
 
 
+def gather_kernel(count, mine, everyone, send_sem, recv_sem):
+    me = lax.axis_index("shard")
+    barrier = pltpu.get_barrier_semaphore()
+    for step in range(1, count):
+        pl.semaphore_signal(barrier, inc=1, device_id={"shard": lax.rem(me + step, count)},
+                            device_id_type=pl.DeviceIdType.MESH)
+    pl.semaphore_wait(barrier, count - 1)
+    copies = []
+    for step in range(1, count):
+        copy = pltpu.make_async_remote_copy(
+            src_ref=mine,
+            dst_ref=everyone.at[:, me],
+            send_sem=send_sem.at[step - 1],
+            recv_sem=recv_sem.at[step - 1],
+            device_id={"shard": lax.rem(me + step, count)},
+            device_id_type=pl.DeviceIdType.MESH,
+        )
+        copy.start()
+        copies.append(copy)
+    for local_step in range(mine.shape[0]):
+        everyone[local_step, me] = mine[local_step]
+    for copy in copies:
+        copy.wait()
+
+
+def gather_tokens(tokens):
+    count = lax.axis_size("shard")
+    steps, part, width = tokens.shape
+    everyone = pl.pallas_call(
+        functools.partial(gather_kernel, count),
+        out_shape=jax.ShapeDtypeStruct((steps, count, part, width), tokens.dtype),
+        in_specs=[pl.BlockSpec(memory_space=pltpu.VMEM)],
+        out_specs=pl.BlockSpec(memory_space=pltpu.VMEM),
+        scratch_shapes=[
+            pltpu.SemaphoreType.DMA((count - 1,)),
+            pltpu.SemaphoreType.DMA((count - 1,)),
+        ],
+        compiler_params=pltpu.CompilerParams(collective_id=1, has_side_effects=True),
+    )(tokens)
+    return everyone.reshape(steps, count * part, width)
+
+
+def tile_rows(rows):
+    return max(tile for tile in range(16, 401, 16) if rows % tile == 0)
+
+
+def steps_kernel(params, momentum, inputs, flipped, wanted, weight, moment, half):
+    rows = params.shape[0]
+    tile = tile_rows(rows)
+    scaling = 1.0 / float(rows) ** 0.5
+    slope_scale = (2.0 / jnp.pi) ** 0.5
+
+    def first(i, carry):
+        at = pl.ds(pl.multiple_of(i * tile, tile), tile)
+        half[at] = params[at].astype(jnp.bfloat16)
+        return carry
+
+    lax.fori_loop(0, rows // tile, first, 0)
+    for local_step in range(inputs.shape[0]):
+        pre = jnp.dot(inputs[local_step], half[...], preferred_element_type=jnp.float32) * scaling
+        square = pre * pre
+        bend = jnp.tanh(slope_scale * pre * (1.0 + 0.044715 * square))
+        cdf = 0.5 * (1.0 + bend)
+        slope = cdf + (0.5 * slope_scale) * pre * (1.0 - bend * bend) * (1.0 + 3.0 * 0.044715 * square)
+        error = pre * cdf - wanted[local_step].astype(jnp.float32)
+        hidden_grad = (error * slope * scaling).astype(jnp.bfloat16)
+        old_weight, old_moment = (params, momentum) if local_step == 0 else (weight, moment)
+
+        def update(i, carry):
+            at = pl.ds(pl.multiple_of(i * tile, tile), tile)
+            gradient = jnp.dot(flipped[local_step, at], hidden_grad, preferred_element_type=jnp.float32)
+            new_moment = momentum_decay * old_moment[at] + gradient
+            new_weight = old_weight[at] - learn_rate * new_moment
+            moment[at] = new_moment
+            weight[at] = new_weight
+            if local_step + 1 < inputs.shape[0]:
+                half[at] = new_weight.astype(jnp.bfloat16)
+            return carry
+
+        lax.fori_loop(0, rows // tile, update, 0)
+
+
+def local_steps(params, momentum, inputs, wanted):
+    rows, columns = params.shape
+    steps, count, _ = inputs.shape
+    block = min(256, columns)
+    column = pl.BlockSpec((rows, block), lambda j: (0, j))
+    out = jax.ShapeDtypeStruct((rows, columns), jnp.float32)
+    return pl.pallas_call(
+        steps_kernel,
+        grid=(pl.cdiv(columns, block),),
+        out_shape=(out, out),
+        in_specs=[
+            column,
+            column,
+            pl.BlockSpec((steps, count, rows), lambda j: (0, 0, 0)),
+            pl.BlockSpec((steps, rows, count), lambda j: (0, 0, 0)),
+            pl.BlockSpec((steps, count, block), lambda j: (0, 0, j)),
+        ],
+        out_specs=(column, column),
+        scratch_shapes=[pltpu.VMEM((rows, block), jnp.bfloat16)],
+        compiler_params=pltpu.CompilerParams(
+            dimension_semantics=("arbitrary",), vmem_limit_bytes=60 * 1024 * 1024
+        ),
+    )(params, momentum, inputs, jnp.swapaxes(inputs, 1, 2), wanted)
+
+
 def local(params, momentum, tokens, targets, blend_weight):
-    inputs = lax.all_gather(tokens[0], "shard", axis=1, tiled=True)
-    wanted = targets[0]
-    weight = params[0]
-    moment = momentum[0]
-    scaling = 1.0 / jnp.sqrt(jnp.float32(weight.shape[0]))
-    for local_step in range(inputs.shape[0]):
-        weight_half = weight.astype(jnp.bfloat16)
-        pre = jnp.dot(inputs[local_step], weight_half, preferred_element_type=jnp.float32) * scaling
-        activation, pullback = jax.vjp(gelu_tanh, pre)
-        (slope,) = pullback(activation - wanted[local_step].astype(jnp.float32))
-        hidden_grad = (slope * scaling).astype(jnp.bfloat16)
-        gradient = lax.dot_general(
-            inputs[local_step],
-            hidden_grad,
-            (((0,), (0,)), ((), ())),
-            preferred_element_type=jnp.float32,
-        )
-        moment = momentum_decay * moment + gradient
-        weight = weight - learn_rate * moment
+    inputs = gather_tokens(tokens[0])
+    weight, moment = local_steps(params[0], momentum[0], inputs, targets[0])
     averaged, mean_moment = replica_means(weight, moment)
     blended = blend_weight * mean_moment + (1.0 - blend_weight) * moment
     return (averaged, blended[None])

time: 273 us -> 231 us (0.85)
  matrix products: 39.6 us -> 0 us
  Pallas kernels: 170 us -> 202 us
  other arithmetic: 34.3 us -> 19.1 us
  waiting for transfers between devices: 13.9 us -> 0 us
  between operations: 14 us -> 0.66 us
  local copies, waits for them, and re-layouts: 0.01 us -> 9.4 us
    dot_general x2 -> x0, matrix products: 39.6 us -> none  [local(): lax.dot_general(inputs[local_step], hidden_grad, (((0,), (0,)), ((), ()))...]
    pallas_call x0 -> x2, Pallas kernels: none -> 30.8 us  [the longest x1 26 us: local_steps(): pl.pallas_call(steps_kernel, grid=(pl.cdiv(columns, block),), out_shape=(...]
    reshape x1 -> x0, other arithmetic: 15.2 us -> none  [replica_means(): weight.reshape(shape)]
    all_gather x1 -> x0, waiting for transfers between devices: 13.2 us -> none  [local(): inputs = lax.all_gather(tokens[0], 'shard', axis=1, tiled=True)]
    unnamed x6 -> x4, local copies, waits for them, and re-layouts: 0.01 us -> 5.77 us
    reshape x0 -> x1, local copies, waits for them, and re-layouts: none -> 3.64 us  [gather_tokens(): return everyone.reshape(steps, count * part, width)]
  transfers between devices with their start and end apart: 1 -> 0, of which waited for: 1 -> 0; matrix products, arithmetic and copies ran while one was open for 0% -> 0% of each run, Pallas kernels for 0% -> 0%
where the time goes in v2:
time: 231 us
  Pallas kernels  202 us (87%)
  other arithmetic  19.1 us (8%)
  local copies, waits for them, and re-layouts  9.4 us (4%)
    pallas_call x1, Pallas kernels, replica_means(): pl.pallas_call(functools.partial(mean_kernel, n, bits, chunks), out_shape...  171 us
    pallas_call x1, Pallas kernels, local_steps(): pl.pallas_call(steps_kernel, grid=(pl.cdiv(columns, block),), out_shape=(...  26 us
    broadcast_in_dim x1, other arithmetic, local(): return (averaged, blended[None])  11.1 us
    convert_element_type x1, other arithmetic, replica_means(): mean.reshape(rows, columns).astype(jnp.float32)  7.33 us
    unnamed x4, local copies, waits for them, and re-layouts  5.77 us
    pallas_call x1, Pallas kernels, gather_tokens(): pl.pallas_call(functools.partial(gather_kernel, count), out_shape=jax.Sha...  4.86 us

profile of v2, /device:TPU:0, one launch (start us, length us, event | category | flops | bytes accessed | tf_op | source)
XLA Modules:
  0.0 230.8 jit_solution(15509178595859886157)
XLA Ops:
  0.6 0.7 broadcast_subtract_fusion
  1.3 2.2 copy.7
  3.5 4.9 %shard_map.68 = bf16[2,2,128,1600]{3,2,1,0:T(8,128)(2,1)} custom-call(bf16[2,128,1600]{2,1,0:T(8,128)(2,1)} %bitcast.24), custom_call_target="tpu_custom_call" | custom-call | tf_op jit(solution)/shard_map/pallas_call | solution.py:223
  8.4 3.6 %copy.11 = bf16[2,256,1600]{1,2,0:T(8,128)(2,1)} copy(bf16[2,256,1600]{2,1,0:T(8,128)(2,1)} %bitcast.17) | data formatting | bytes 3276800 | tf_op jit(solution)/shard_map/reshape | solution.py:234
  12.0 3.6 %copy.9 = bf16[1,2,256,1600]{3,2,1,0:T(8,128)(2,1)} copy(bf16[1,2,256,1600]{2,3,1,0:T(8,128)(2,1)} %param.8) | data formatting | bytes 3276800 | tf_op args[3]
  15.6 26.0 %shard_map.69 = (f32[1600,1600]{1,0:T(8,128)}, f32[1600,1600]{1,0:T(8,128)}) custom-call(f32[1600,1600]{1,0:T(8,128)} %bitcast.19, f32[1600,1600]{1,0:T(8,128)} %bitcast.20, bf16[2,256,1600]{2,1,0:T(8,128)(2,1)} %bitcast.18, bf16[2,1600,256]{2,1,0:T(8,128)(2,1)} %bitcast.23, bf16[2,256,1600]{2,1,0:T(8,128)(2,1)} %bitcast.22), custom_call_target="tpu_custom_call" | custom-call | tf_op jit(solution)/shard_map/pallas_call | solution.py:283
  41.6 0.0 copy-start
  41.6 170.8 %shard_map.70 = (bf16[200,8,1600]{2,1,0:T(8,128)(2,1)}, bf16[200,8,1600]{2,1,0:T(8,128)(2,1)}) custom-call(f32[200,8,1600]{2,1,0:T(8,128)} %bitcast.21, f32[200,8,1600]{2,1,0:T(8,128)} %bitcast.16), custom_call_target="tpu_custom_call" | custom-call | bytes 19200000 | tf_op jit(solution)/shard_map/pallas_call | solution.py:172
  212.4 0.0 copy-done
  212.4 11.1 %fusion.1 = f32[1,1600,1600]{2,1,0:T(8,128)} fusion(f32[1600,1600]{1,0:T(8,128)} %get-tuple-element.7, bf16[200,8,1600]{2,1,0:T(8,128)(2,1)} %get-tuple-element.9, f32[1600]{0:T(1024)S(1)} %broadcast_subtract_fusion, f32[1600]{0:T(1024)S(1)} %copy-done), kind=kLoop, calls=%fused_computation.2 | loop fusion | flops 10240000 | bytes 25612800 | tf_op jit(solution)/shard_map/broadcast_in_dim | solution.py:307
  223.4 7.3 %bitcast_convert_fusion = f32[1600,1600]{1,0:T(8,128)} fusion(bf16[200,8,1600]{2,1,0:T(8,128)(2,1)} %get-tuple-element.8), kind=kLoop, calls=%fused_computation.3 | loop fusion | flops 2560000 | bytes 15360000 | tf_op jit(solution)/shard_map/convert_element_type | solution.py:192
Async XLA Ops:
  41.6 170.8 %copy-start = (f32[1600]{0:T(1024)S(1)}, f32[1600]{0:T(1024)}, u32[]{:S(2)}) copy-start(f32[1600]{0:T(1024)} %param.9) | copy-start | bytes 19204

commit v3 on v2

--- a/solution.py
+++ b/solution.py
@@ -38,6 +38,7 @@
     sources, sinks = (weight_hbm, moment_hbm), (out_w_hbm, out_m_hbm)
     split = weight_hbm.shape[0]
     total = 2 * split
+    size = n // 2
 
     def side(bit):
         return (me // (1 << bit)) % 2
@@ -48,16 +49,16 @@
     loads = []
     for chunk in range(chunks):
         mine = []
-        for which, at, offset, count in pieces(chunk * n, n, split, total):
+        for which, at, offset, count in pieces(chunk * size, size, split, total):
             mine.append(pltpu.make_async_copy(
                 sources[which].at[pl.ds(at, count)],
-                held.at[pl.ds(chunk * n + offset, count)],
+                held.at[pl.ds(chunk * size + offset, count)],
                 load_sem.at[chunk, which],
             ))
         for copy in mine:
             copy.start()
         loads.append(mine)
-    padding = chunks * n - total
+    padding = chunks * size - total
     if padding:
         held[pl.ds(total, padding)] = jnp.zeros((padding,) + held.shape[1:], held.dtype)
 
@@ -68,10 +69,25 @@
     pl.semaphore_wait(barrier, bits)
 
     copies = {}
-    low = {chunk: [chunk * n] for chunk in range(chunks)}
+    low = {chunk: [chunk * size] for chunk in range(chunks)}
+
+    last = 2 * bits - 1
+
+    def send(chunk, stage, bit, src, dst):
+        copy = pltpu.make_async_remote_copy(
+            src_ref=src,
+            dst_ref=dst,
+            send_sem=send_sem.at[chunk, stage],
+            recv_sem=recv_sem.at[chunk, stage],
+            device_id={"rep": partner(bit)},
+            device_id_type=pl.DeviceIdType.MESH,
+        )
+        copy.start()
+        copies[chunk, stage] = copy
 
     def act(chunk, stage):
         order = bit_order(chunk, bits)
+        first = chunk * size
         if stage == 0:
             for copy in loads[chunk]:
                 copy.wait()
@@ -79,21 +95,19 @@
             copies[chunk, stage - 1].wait_recv()
         if stage < bits:
             bit = order[stage]
-            half = n >> (stage + 1)
+            swap = stage == bits - 1
+            half = 1 if swap else size >> (stage + 1)
             start = low[chunk][stage]
-            keep = start + side(bit) * half
-            give = start + (1 - side(bit)) * half
-            slot = chunk * n + (n - 2 * half)
-            before = slot - 2 * half
+            keep = start if swap else start + side(bit) * half
+            give = start if swap else start + (1 - side(bit)) * half
+            slot = first + (size - 1 if swap else size - 2 * half)
+            before = first + size - 2 * (size >> stage)
 
             def step(i, carry):
-                if stage == 0:
-                    staged[slot + i] = held[give + i].astype(jnp.bfloat16)
-                else:
-                    staged[slot + i] = (
-                        held[give + i]
-                        + landed[before + (give - start) + i].astype(jnp.float32)
-                    ).astype(jnp.bfloat16)
+                value = held[give + i]
+                if stage > 0:
+                    value = value + landed[before + (give - start) + i].astype(jnp.float32)
+                staged[slot + i] = value.astype(jnp.bfloat16)
                 return carry
 
             def keep_step(i, carry):
@@ -101,43 +115,23 @@
                 return carry
 
             lax.fori_loop(0, half, step, 0)
-            copy = pltpu.make_async_remote_copy(
-                src_ref=staged.at[pl.ds(slot, half)],
-                dst_ref=landed.at[pl.ds(slot, half)],
-                send_sem=send_sem.at[chunk, stage],
-                recv_sem=recv_sem.at[chunk, stage],
-                device_id={"rep": partner(bit)},
-                device_id_type=pl.DeviceIdType.MESH,
-            )
-            copy.start()
-            copies[chunk, stage] = copy
-            if stage > 0:
+            send(chunk, stage, bit, staged.at[pl.ds(slot, half)], landed.at[pl.ds(slot, half)])
+            if stage > 0 and not swap:
                 lax.fori_loop(0, half, keep_step, 0)
             low[chunk].append(keep)
-        elif stage < 2 * bits:
-            back = 2 * bits - 1 - stage
-            bit = order[back]
-            size = n >> (back + 1)
-            start = low[chunk][back + 1]
-            if stage == bits:
-                slot = chunk * n + n - 2
-                result[start] = (
-                    (held[start] + landed[slot].astype(jnp.float32)) * (1.0 / n)
-                ).astype(jnp.bfloat16)
-            copy = pltpu.make_async_remote_copy(
-                src_ref=result.at[pl.ds(start, size)],
-                dst_ref=result.at[pl.ds(start, size)],
-                send_sem=send_sem.at[chunk, stage],
-                recv_sem=recv_sem.at[chunk, stage],
-                device_id={"rep": partner(bit)},
-                device_id_type=pl.DeviceIdType.MESH,
-            )
-            copy.start()
-            copies[chunk, stage] = copy
+            return
+        if stage == bits:
+            slot = first + size - 1
+            both = staged[slot].astype(jnp.float32) + landed[slot].astype(jnp.float32)
+            result[low[chunk][bits - 1]] = (both * (1.0 / n)).astype(jnp.bfloat16)
+        if stage < last:
+            back = last - 1 - stage
+            held_now = pl.ds(low[chunk][back + 1], size >> (back + 1))
+            send(chunk, stage, order[back], result.at[held_now], result.at[held_now])
         else:
-            for which, at, offset, count in pieces(chunk * n, n, split, total):
+            for which, at, offset, count in pieces(first, size, split, total):
                 copy = pltpu.make_async_copy(
-                    result.at[pl.ds(chunk * n + offset, count)],
+                    result.at[pl.ds(first + offset, count)],
                     sinks[which].at[pl.ds(at, count)],
                     store_sem.at[chunk, which],
                 )
@@ -146,8 +140,8 @@
 
     stores = []
     waves = -(-chunks // 3)
-    for tick in range(waves + 2 * bits):
-        for stage in range(2 * bits, -1, -1):
+    for tick in range(waves + last):
+        for stage in range(last, -1, -1):
             wave = tick - stage
             if 0 <= wave < waves:
                 for chunk in range(3 * wave, min(3 * wave + 3, chunks)):
@@ -164,8 +158,8 @@
     assert n == 1 << bits
     rows, columns = weight.shape
     slabs = rows // ROWS
-    chunks = -(-2 * slabs // n)
-    space = chunks * n
+    chunks = -(-2 * slabs // (n // 2))
+    space = chunks * (n // 2)
     shape = (slabs, ROWS, columns)
     out = jax.ShapeDtypeStruct(shape, jnp.bfloat16)
     sent = chunks * 2 * (n - 1) * ROWS * columns * 2
@@ -180,8 +174,8 @@
             pltpu.VMEM((space, ROWS, columns), jnp.bfloat16),
             pltpu.VMEM((space, ROWS, columns), jnp.bfloat16),
             pltpu.SemaphoreType.DMA((chunks, 2)),
-            pltpu.SemaphoreType.DMA((chunks, 2 * bits)),
-            pltpu.SemaphoreType.DMA((chunks, 2 * bits)),
+            pltpu.SemaphoreType.DMA((chunks, 2 * bits - 1)),
+            pltpu.SemaphoreType.DMA((chunks, 2 * bits - 1)),
             pltpu.SemaphoreType.DMA((chunks, 2)),
         ],
         compiler_params=pltpu.CompilerParams(

time: 231 us -> 233 us (level)
  no operation moved by 1% of the time
where the time goes in v3:
time: 233 us; the launch traced here: 232 us
  Pallas kernels  203 us (87%)
  other arithmetic  19.1 us (8%)
  local copies, waits for them, and re-layouts  9.4 us (4%)
    pallas_call x1, Pallas kernels, replica_means(): pl.pallas_call(functools.partial(mean_kernel, n, bits, chunks), out_shape...  172 us
    pallas_call x1, Pallas kernels, local_steps(): pl.pallas_call(steps_kernel, grid=(pl.cdiv(columns, block),), out_shape=(...  26 us
    broadcast_in_dim x1, other arithmetic, local(): return (averaged, blended[None])  11.1 us
    convert_element_type x1, other arithmetic, replica_means(): mean.reshape(rows, columns).astype(jnp.float32)  7.33 us
    unnamed x4, local copies, waits for them, and re-layouts  5.77 us
    pallas_call x1, Pallas kernels, gather_tokens(): pl.pallas_call(functools.partial(gather_kernel, count), out_shape=jax.Sha...  4.86 us

profile of v3, /device:TPU:0, one launch (start us, length us, event | category | flops | bytes accessed | tf_op | source)
XLA Modules:
  0.0 232.3 jit_solution(12736168941358144159)
XLA Ops:
  0.6 0.7 broadcast_subtract_fusion
  1.3 2.2 copy.7
  3.5 4.9 %shard_map.68 = bf16[2,2,128,1600]{3,2,1,0:T(8,128)(2,1)} custom-call(bf16[2,128,1600]{2,1,0:T(8,128)(2,1)} %bitcast.24), custom_call_target="tpu_custom_call" | custom-call | tf_op jit(solution)/shard_map/pallas_call | solution.py:217
  8.4 3.6 %copy.11 = bf16[2,256,1600]{1,2,0:T(8,128)(2,1)} copy(bf16[2,256,1600]{2,1,0:T(8,128)(2,1)} %bitcast.17) | data formatting | bytes 3276800 | tf_op jit(solution)/shard_map/reshape | solution.py:228
  12.0 3.6 %copy.9 = bf16[1,2,256,1600]{3,2,1,0:T(8,128)(2,1)} copy(bf16[1,2,256,1600]{2,3,1,0:T(8,128)(2,1)} %param.8) | data formatting | bytes 3276800 | tf_op args[3]
  15.6 26.0 %shard_map.69 = (f32[1600,1600]{1,0:T(8,128)}, f32[1600,1600]{1,0:T(8,128)}) custom-call(f32[1600,1600]{1,0:T(8,128)} %bitcast.19, f32[1600,1600]{1,0:T(8,128)} %bitcast.20, bf16[2,256,1600]{2,1,0:T(8,128)(2,1)} %bitcast.18, bf16[2,1600,256]{2,1,0:T(8,128)(2,1)} %bitcast.23, bf16[2,256,1600]{2,1,0:T(8,128)(2,1)} %bitcast.22), custom_call_target="tpu_custom_call" | custom-call | tf_op jit(solution)/shard_map/pallas_call | solution.py:277
  41.6 0.0 copy-start
  41.6 172.3 %shard_map.70 = (bf16[200,8,1600]{2,1,0:T(8,128)(2,1)}, bf16[200,8,1600]{2,1,0:T(8,128)(2,1)}) custom-call(f32[200,8,1600]{2,1,0:T(8,128)} %bitcast.21, f32[200,8,1600]{2,1,0:T(8,128)} %bitcast.16), custom_call_target="tpu_custom_call" | custom-call | bytes 38400000 | tf_op jit(solution)/shard_map/pallas_call | solution.py:166
  213.9 0.0 copy-done
  213.9 11.1 %fusion.1 = f32[1,1600,1600]{2,1,0:T(8,128)} fusion(f32[1600,1600]{1,0:T(8,128)} %get-tuple-element.7, bf16[200,8,1600]{2,1,0:T(8,128)(2,1)} %get-tuple-element.9, f32[1600]{0:T(1024)S(1)} %broadcast_subtract_fusion, f32[1600]{0:T(1024)S(1)} %copy-done), kind=kLoop, calls=%fused_computation.2 | loop fusion | flops 10240000 | bytes 25612800 | tf_op jit(solution)/shard_map/broadcast_in_dim | solution.py:301
  225.0 7.3 %bitcast_convert_fusion = f32[1600,1600]{1,0:T(8,128)} fusion(bf16[200,8,1600]{2,1,0:T(8,128)(2,1)} %get-tuple-element.8), kind=kLoop, calls=%fused_computation.3 | loop fusion | flops 2560000 | bytes 15360000 | tf_op jit(solution)/shard_map/convert_element_type | solution.py:186
Async XLA Ops:
  41.6 172.3 %copy-start = (f32[1600]{0:T(1024)S(1)}, f32[1600]{0:T(1024)}, u32[]{:S(2)}) copy-start(f32[1600]{0:T(1024)} %param.9) | copy-start | bytes 19204
